TPU v7x, 32 devices: a whole 2x2x4 slice. The times are simulated.
32 devices in a mesh: seq: 8 (over z, y), chan: 4 (over x, core).
Axes of the slice: x: 2, y: 2, z: 4, core: 2. Of those that a mesh axis runs over, the one named last changes fastest.
Arguments:
- hidden_in: bfloat16 [1024, 2048], P('seq', 'chan'), may hold values from -6 to 6
- norm_gain: float32 [2048], replicated, may hold values from 0.5 to 1.5
- in_weight: bfloat16 [2048, 2, 4096], P('seq', None, 'chan'), may hold values from -0.125 to 0.125
- conv_weight: float32 [2, 4, 4096], P(None, None, 'chan'), may hold values from -3 to 3
- conv_bias: float32 [2, 4096], P(None, 'chan'), may hold values from -0.5 to 0.5
- proj_weight: bfloat16 [2, 4096, 160], P(None, 'chan'), may hold values from -0.1875 to 0.1875
- step_weight: bfloat16 [2, 128, 4096], P(None, None, 'chan'), may hold values from -0.5 to 0.5
- decay_rate: float32 [2, 4096], P(None, 'chan'), may hold values from 0.00024414062 to 0.25
- skip_gain: float32 [2, 4096], P(None, 'chan'), may hold values from 0.5 to 1.5
- out_weight: bfloat16 [4096, 2048], P('chan', 'seq'), may hold values from -0.09375 to 0.09375
Outputs:
- mixed: bfloat16 [1024, 2048], P('seq', 'chan')
All inputs are finite; a program needn't handle non-finite values.
Results may differ from a plain program's by a relative error of at most 0.0095.
Values may be sent and summed in bfloat16 or wider, within the bound.
No kernel may reach another device: no remote copies, remote signals or barrier semaphores. Data moves between devices by JAX's collectives and lax.ppermute only.
A program may use at most 128 MiB of HBM per device.

v0:
```python
import jax
import jax.numpy as jnp
from jax import lax
from jax.sharding import PartitionSpec as P

STATE = 16
WIDTH = 4


def with_halo(block, sides, width):
    for axis, dim in sides:
        count = lax.axis_size(axis)
        forward = [(i, i + 1) for i in range(count - 1)]
        backward = [(target, source) for source, target in forward]
        low = lax.ppermute(
            lax.slice_in_dim(block, block.shape[dim] - width, None, axis=dim), axis, forward
        )
        high = lax.ppermute(lax.slice_in_dim(block, 0, width, axis=dim), axis, backward)
        block = jnp.concatenate([low, block, high], axis=dim)
    return block


def entering(array, axis, combine, identity, reverse):
    devices, here = (lax.axis_size(axis), lax.axis_index(axis))
    everything = jax.tree.map(lambda part: lax.all_gather(part, axis), array)
    start = jax.tree.map(
        lambda part, zero: jnp.broadcast_to(jnp.asarray(zero, part.dtype), part.shape),
        array,
        identity,
    )

    def hop(k, before):
        at = devices - 1 - k if reverse else k
        reached = at > here if reverse else at < here
        new = combine(before, jax.tree.map(lambda part: part[at], everything))
        return jax.tree.map(lambda a, b: jnp.where(reached, a, b), new, before)

    return lax.fori_loop(0, devices, hop, start)


def conv_taps(padded, conv_weight, conv_bias, length):
    reach = conv_weight.shape[1] - 1
    forward = jnp.zeros((length, padded.shape[1]), jnp.float32) + conv_bias[0][None, :]
    backward = jnp.zeros((length, padded.shape[1]), jnp.float32) + conv_bias[1][None, :]
    for offset in range(reach + 1):
        forward = forward + conv_weight[0, offset][None, :] * padded[offset : offset + length]
        begin = 2 * reach - offset
        backward = backward + conv_weight[1, offset][None, :] * padded[begin : begin + length]
    return jax.nn.silu(jnp.stack([forward, backward])).astype(jnp.bfloat16)


def sweep(drive_values, key_rows, query_rows, epsilon, initial, reverse, keeping):
    product = jnp.ones(initial.shape, jnp.float32)

    def advance(carry, current):
        product, state = carry
        drive_row, key_row, query_row, eps_row = current
        decay = 1.0 - eps_row[None, :] * (key_row * key_row)[:, None]
        state = decay * state + key_row[:, None] * (eps_row * drive_row)[None, :]
        product = decay * product
        if keeping == "reads":
            output = jnp.sum(query_row[:, None] * state, axis=0)
        else:
            output = None
        return ((product, state), output)

    (product, state), outputs = lax.scan(
        advance,
        (product, initial),
        (drive_values, key_rows, query_rows, epsilon),
        reverse=reverse,
        unroll=16,
    )
    return (product, state, outputs)


def combine(earlier, latter):
    return (latter[0] * earlier[0], latter[0] * earlier[1] + latter[1])


def per_device(
    hidden_in,
    norm_gain,
    in_weight,
    conv_weight,
    conv_bias,
    proj_weight,
    step_weight,
    decay_rate,
    skip_gain,
    out_weight,
):
    gathered = lax.all_gather(hidden_in, "chan", axis=1, tiled=True).astype(jnp.float32)
    normed = (
        gathered
        * lax.rsqrt(jnp.mean(gathered * gathered, axis=1, keepdims=True) + 1e-05)
        * norm_gain[None, :]
    ).astype(jnp.bfloat16)
    row_count = normed.shape[0]
    channels = in_weight.shape[2]
    piece = lax.all_gather(in_weight, "seq", axis=0, tiled=True)
    projected = jnp.dot(
        normed, piece.reshape(piece.shape[0], 2 * channels), preferred_element_type=jnp.float32
    )
    projected = projected.astype(jnp.bfloat16).reshape(row_count, 2, channels)
    branch = projected[:, 0, :]
    gate_half = projected[:, 1, :].astype(jnp.float32)
    padded = with_halo(branch, (("seq", 0),), WIDTH - 1).astype(jnp.float32)
    driven = conv_taps(padded, conv_weight, conv_bias, row_count)
    partial_value = jnp.einsum(
        "dte,def->tdf", driven, proj_weight, preferred_element_type=jnp.float32
    )
    features = lax.psum(partial_value, "chan")
    key_rows = features[:, :, :STATE]
    query_rows = features[:, :, STATE : 2 * STATE]
    low_rank = features[:, :, 2 * STATE :].astype(jnp.bfloat16)
    step_size = jnp.einsum(
        "tdr,dre->tde", low_rank, step_weight, preferred_element_type=jnp.float32
    )
    beta_rows = 2.0 * decay_rate[None, :, :] * jax.nn.sigmoid(step_size)
    epsilon = beta_rows / (1.0 + beta_rows * jnp.sum(key_rows * key_rows, axis=2, keepdims=True))
    drive_values = driven.astype(jnp.float32)
    zero_state = jnp.zeros((STATE, channels), jnp.float32)
    keeping = "summary"
    passes = [
        sweep(
            drive_values[direction],
            key_rows[:, direction],
            query_rows[:, direction],
            epsilon[:, direction],
            zero_state,
            direction == 1,
            keeping,
        )
        for direction in range(2)
    ]
    identity = (jnp.ones((STATE, channels), jnp.float32), zero_state)
    incoming_forward = entering((passes[0][0], passes[0][1]), "seq", combine, identity, False)[1]
    incoming_reverse = entering((passes[1][0], passes[1][1]), "seq", combine, identity, True)[1]
    incoming = [incoming_forward, incoming_reverse]
    total = jnp.zeros((row_count, channels), jnp.float32)
    for direction in range(2):
        reads = sweep(
            drive_values[direction],
            key_rows[:, direction],
            query_rows[:, direction],
            epsilon[:, direction],
            incoming[direction],
            direction == 1,
            "reads",
        )[2]
        total = total + reads + skip_gain[direction][None, :] * drive_values[direction]
    combined = (total * jax.nn.silu(gate_half)).astype(jnp.bfloat16)
    partial_out = jnp.dot(
        combined,
        lax.all_gather(out_weight, "seq", axis=1, tiled=True),
        preferred_element_type=jnp.float32,
    )
    summed = lax.psum(partial_out, "chan")
    share_width = summed.shape[1] // lax.axis_size("chan")
    share = lax.dynamic_slice_in_dim(summed, lax.axis_index("chan") * share_width, share_width, 1)
    return share.astype(jnp.bfloat16)


def solution(mesh):
    in_specs = (
        P("seq", "chan"),
        P(),
        P("seq", None, "chan"),
        P(None, None, "chan"),
        P(None, "chan"),
        P(None, "chan", None),
        P(None, None, "chan"),
        P(None, "chan"),
        P(None, "chan"),
        P("chan", "seq"),
    )
    out_specs = P("seq", "chan")
    return jax.shard_map(
        per_device, mesh=mesh, in_specs=in_specs, out_specs=out_specs, check_vma=False
    )
```

profile of v0, /device:TPU:0, one launch (start us, length us, event | category | flops | bytes accessed | tf_op | source)
XLA Modules:
  0.0 489.7 jit_solution(10717089666315897083)
XLA Ops:
  7.3 8.9 %all_gather.33 = bf16[128,2048]{1,0:T(8,128)(2,1)S(1)} all-gather(bf16[128,512]{1,0:T(8,128)(2,1)} %param.22), channel_id=1, replica_groups=mesh['seq'=8,'chan'=4] {'chan'}, dimensions={1}, use_global_device_ids=true | all-gather | bytes 655360 | tf_op jit(solution)/shard_map/all_gather | solution.py:93
  18.1 118.6 %all-gather.7.cloned.1.call-done = bf16[2048,2,1024]{2,1,0:T(2,128)(2,1)} async-done(((bf16[256,2,1024]{2,1,0:T(2,128)(2,1)}), bf16[2048,2,1024]{2,1,0:T(2,128)(2,1)}) %all-gather.7.cloned.1.call-update) | async-done | bytes 8388624 | tf_op jit(solution)/shard_map/all_gather | solution.py:101
  136.7 10.1 %copy.42 = bf16[256,8,2,1024]{3,1,2,0:T(8,128)(2,1)} copy(bf16[256,8,2,1024]{3,2,1,0:T(2,128)(2,1)} %bitcast.855) | data formatting | bytes 16777216
  146.8 4.7 convolution_convert_fusion
  153.3 4.5 collective-permute-start
  163.2 30.7 %all-reduce.3.cloned.1.call-done = f32[128,2,160]{0,2,1:T(8,128)} async-done(((f32[128,2,160]{0,2,1:T(8,128)}), f32[128,2,160]{0,2,1:T(8,128)}) %all-reduce.3.cloned.1.call-update) | async-done | bytes 163856 | tf_op jit(solution)/shard_map/psum | solution.py:113
  199.1 22.7 %while.92 = (s32[]{:T(128)}, f32[16,1024]{1,0:T(8,128)S(1)}, f32[16,1024]{1,0:T(8,128)S(1)}, f32[8,16,1024]{2,1,0:T(8,128)}, f32[8,16,16]{2,1,0:T(8,128)S(1)}, /...) while((s32[]{:T(128)}, f32[16,1024]{1,0:T(8,128)S(1)}, ...), condition=%wide.region_26.27_spmd.clone, body=%wide.region_25.26_spmd.clone.sunk | while | flops 2146579 | bytes 924200 | solution.py:67
  199.1 2.0 constant_dynamic-slice_fusion.231
  202.1 2.0 constant_dynamic-slice_fusion.231
  210.6 2.0 constant_dynamic-slice_fusion.231
  221.8 9.5 %while.90 = (s32[]{:T(128)}, f32[16,1024]{1,0:T(8,128)S(1)}, f32[16,1024]{1,0:T(8,128)S(1)}, f32[8,16,1024]{2,1,0:T(8,128)S(1)}, f32[8,16,16]{2,1,0:T(8,128)S(1)...) while((s32[]{:T(128)}, f32[16,1024]{1,0:T(8,128)S(1)}, ...), condition=%wide.region_4.5_spmd.clone, body=%wide.region_3.4_spmd.clone.sunk | while | flops 2146578 | bytes 924180 | solution.py:67
  231.3 37.0 %all-gather.1 = f32[128,1024]{1,0:T(8,128)} all-gather(f32[16,1024]{1,0:T(8,128)S(1)} %get-tuple-element.566), channel_id=3, replica_groups=mesh['seq'=8,'chan'=4] {'seq'}, dimensions={0}, use_global_device_ids=true | all-gather | bytes 589824 | tf_op jit(solution)/shard_map/all_gather | solution.py:25
  268.3 34.7 %all-gather.3 = f32[128,1024]{1,0:T(8,128)} all-gather(f32[16,1024]{1,0:T(8,128)S(1)} %get-tuple-element.570), channel_id=5, replica_groups=mesh['seq'=8,'chan'=4] {'seq'}, dimensions={0}, use_global_device_ids=true | all-gather | bytes 589824 | tf_op jit(solution)/shard_map/all_gather | solution.py:25
  303.0 33.4 %all-gather = f32[128,1024]{1,0:T(8,128)} all-gather(f32[16,1024]{1,0:T(8,128)S(1)} %get-tuple-element.565), channel_id=2, replica_groups=mesh['seq'=8,'chan'=4] {'seq'}, dimensions={0}, use_global_device_ids=true | all-gather | bytes 589824 | tf_op jit(solution)/shard_map/all_gather | solution.py:25
  336.4 7.5 %while.91 = (s32[]{:T(128)}, f32[16,1024]{1,0:T(8,128)S(1)}, s32[]{:T(128)}, f32[8,16,1024]{2,1,0:T(8,128)}, f32[8,16,1024]{2,1,0:T(8,128)}, /*index=5*/s32[]{:T(128)}, s32[]{:T(128)}) while((s32[]{:T(128)}, f32[16,1024]{1,0:T(8,128)S(1)}, s32[]{:T(128)}, f32[8,16,1024]{2,1,0:T(8,128)}, f32[8,16,1024]{2,1,0:T(8,128)}, ...), condition=%wide.region_6.7_spmd.clone, body=%wide.region_5.6_spmd.clone.sunk | while | flops 65540 | bytes 262253 | solution.py:38
  343.9 33.6 %all-gather.2 = f32[128,1024]{1,0:T(8,128)} all-gather(f32[16,1024]{1,0:T(8,128)S(1)} %get-tuple-element.569), channel_id=4, replica_groups=mesh['seq'=8,'chan'=4] {'seq'}, dimensions={0}, use_global_device_ids=true | all-gather | bytes 589824 | tf_op jit(solution)/shard_map/all_gather | solution.py:25
  377.5 7.5 %while.93 = (s32[]{:T(128)}, f32[16,1024]{1,0:T(8,128)S(1)}, s32[]{:T(128)}, f32[8,16,1024]{2,1,0:T(8,128)}, f32[8,16,1024]{2,1,0:T(8,128)}, /*index=5*/s32[]{:T(128)}, s32[]{:T(128)}, s32[]{:T(128)}, s32[]{:T(128)}) while((s32[]{:T(128)}, f32[16,1024]{1,0:T(8,128)S(1)}, s32[]{:T(128)}, f32[8,16,1024]{2,1,0:T(8,128)}, ...), condition=%wide.region_28.29_spmd.clone, body=%wide.region_27.28_spmd.clone.sunk | while | flops 65544 | bytes 262315 | solution.py:38
  385.9 33.0 %while.89 = (s32[]{:T(128)}, f32[16,1024]{1,0:T(8,128)S(1)}, f32[8,16,1024]{2,1,0:T(8,128)}, f32[8,16,1024]{2,1,0:T(8,128)}, f32[8,16,16]{2,1,0:T(8,128)S(1)}, /...) while((s32[]{:T(128)}, f32[16,1024]{1,0:T(8,128)S(1)}, ...), condition=%wide.region_46.47_spmd, body=%wide.region_29.46_spmd.sunk | while | flops 2408722 | bytes 2033121 | solution.py:67
  386.1 2.0 constant_dynamic-slice_fusion.229
  390.3 2.0 constant_dynamic-slice_fusion.229
  402.6 2.0 constant_dynamic-slice_fusion.229
  418.9 32.4 %while.88 = (s32[]{:T(128)}, f32[16,1024]{1,0:T(8,128)S(1)}, f32[8,16,1024]{2,1,0:T(8,128)S(1)}, f32[8,16,1024]{2,1,0:T(8,128)S(1)}, f32[8,16,16]{2,1,0:T(8,128)...) while((s32[]{:T(128)}, f32[16,1024]{1,0:T(8,128)S(1)}, ...), condition=%wide.region_24.25_spmd, body=%wide.region_7.24_spmd.sunk | while | flops 2490641 | bytes 2106965 | solution.py:67
  452.8 2.9 fusion.342
  455.7 26.7 %all-reduce.4 = bf16[128,2048]{1,0:T(8,128)(2,1)S(1)} all-reduce(f32[128,2048]{1,0:T(8,128)S(1)} %fusion.342), channel_id=1, replica_groups=mesh['seq'=8,'chan'=4] {'chan'}, use_global_device_ids=true, to_apply=%region_47.48 | all-reduce | flops 262144 | bytes 1572864 | tf_op jit(solution)/shard_map/psum | solution.py:159
  (861 shorter events, 112.2 us)
Async XLA Ops:
  6.5 153.8 %copy-start = (bf16[2,1024,160]{1,2,0:T(8,128)(2,1)S(1)}, bf16[2,1024,160]{1,2,0:T(8,128)(2,1)}, u32[]{:S(2)}) copy-start(bf16[2,1024,160]{1,2,0:T(8,128)(2,1)} %param.27) | copy-start | bytes 1966084
  6.5 130.2 %all-gather.7.cloned.1.call-start = ((), (), s32[]{:S(2)}) async-start(), calls=%async_computation | async-start | bytes 9437184 | tf_op jit(solution)/shard_map/all_gather | solution.py:101
  7.3 186.6 %all-reduce.3.cloned.1.call-start = ((), (), s32[]{:S(2)}) async-start(), calls=%async_computation.1 | async-start | bytes 327680 | tf_op jit(solution)/shard_map/psum | solution.py:113
  136.7 10.1 %copy-start.4 = (f32[2048]{0:T(1024)S(1)}, f32[2048]{0:T(1024)}, u32[]{:S(2)}) copy-start(f32[2048]{0:T(1024)} %param.23) | copy-start | bytes 24580
  151.5 10.6 %copy-start.5 = (f32[2,1024]{1,0:T(2,128)S(1)}, f32[2,1024]{1,0:T(2,128)}, u32[]{:S(2)}) copy-start(f32[2,1024]{1,0:T(2,128)} %param.29) | copy-start | bytes 24580
  151.5 10.7 %copy-start.6 = (f32[2,1024]{1,0:T(2,128)S(1)}, f32[2,1024]{1,0:T(2,128)}, u32[]{:S(2)}) copy-start(f32[2,1024]{1,0:T(2,128)} %param.30) | copy-start | bytes 24580
  152.0 7.5 %collective-permute-start.1 = (bf16[3,1024]{1,0:T(4,128)(2,1)S(1)}, bf16[3,1024]{1,0:T(4,128)(2,1)S(1)}, u32[]{:S(2)}, u32[]{:S(2)}) collective-permute-start(bf16[3,1024]{1,0:T(4,128)(2,1)S(1)} %bitcast.1151), channel_id=1, source_target_pairs={{4,0},{8,4},{12,8},{16,12},{20,16},{24,20},{28,24},{5,1},{9,5},{13... | collective-permute-start | bytes 18440 | tf_op jit(solution)/shard_map/ppermute | solution.py:18
  153.3 6.2 %collective-permute-start = (bf16[3,1024]{1,0:T(4,128)(2,1)S(1)}, bf16[3,1024]{1,0:T(4,128)(2,1)S(1)}, u32[]{:S(2)}, u32[]{:S(2)}) collective-permute-start(bf16[3,1024]{1,0:T(4,128)(2,1)S(1)} %bitcast.1150), channel_id=1, source_target_pairs={{0,4},{4,8},{8,12},{12,16},{16,20},{20,24},{24,28},{1,5},{5,9},{9,... | collective-permute-start | bytes 18440 | tf_op jit(solution)/shard_map/ppermute | solution.py:15
  161.4 291.4 %all-gather.9.cloned.1.call-start = ((), (), s32[]{:S(2)}) async-start(), calls=%async_computation.2 | async-start | bytes 4718592 | tf_op jit(solution)/shard_map/all_gather | solution.py:156
  163.2 35.9 %copy-start.1 = (f32[16,1024]{1,0:T(8,128)S(1)}, f32[16,1024]{1,0:T(8,128)}, u32[]{:S(2)}) copy-start(f32[16,1024]{1,0:T(8,128)} %custom-call.4) | copy-start | bytes 196612
  163.2 35.9 %copy-start.2 = (f32[16,1024]{1,0:T(8,128)S(1)}, f32[16,1024]{1,0:T(8,128)}, u32[]{:S(2)}) copy-start(f32[16,1024]{1,0:T(8,128)} %custom-call.3) | copy-start | bytes 196612
  231.3 154.6 %copy-start.3 = (f32[8,16,16]{2,1,0:T(8,128)}, f32[8,16,16]{2,1,0:T(8,128)S(1)}, u32[]{:S(2)}) copy-start(f32[8,16,16]{2,1,0:T(8,128)S(1)} %get-tuple-element.2563) | copy-start | bytes 24580
Sparse Core Ops, SparseCore 0:
  9.5 127.1 all-gather.6
  161.5 32.3 all-reduce.2
  195.9 86.4 all-gather.8
where the time goes:
time: 494 us; the launch traced here: 490 us
  blocking collectives  174 us (35%)
  waiting for transfers between devices  151 us (31%)
  local copies, waits for them, and re-layouts  69.2 us (14%)
  other arithmetic  59.8 us (12%)
  between operations  13.4 us (3%)
  matrix products  10.3 us (2%)
  loops' own time  6.06 us (1%)
  starting transfers between devices  5.92 us (1%)
    all_gather x4, blocking collectives, entering(): everything = jax.tree.map(lambda part: lax.all_gather(part, axis), array)  139 us
    all_gather x1, waiting for transfers between devices, per_device(): piece = lax.all_gather(in_weight, 'seq', axis=0, tiled=True)  119 us
    slice x32, local copies, waits for them, and re-layouts, sweep(): lax.scan(advance, (product, initial), (drive_values, key_rows, query_rows...  34.3 us
    psum x1, waiting for transfers between devices, per_device(): features = lax.psum(partial_value, 'chan')  30.7 us
    psum x1, blocking collectives, per_device(): summed = lax.psum(partial_out, 'chan')  26.7 us
    reduce_sum x136, other arithmetic, advance(): output = jnp.sum(query_row[:, None] * state, axis=0)  17.7 us
    select_n x16, other arithmetic, hop(): return jax.tree.map(lambda a, b: jnp.where(reached, a, b), new, before)  14.6 us
    mul x32, other arithmetic, advance(): decay = 1.0 - eps_row[None, :] * (key_row * key_row)[:, None]  12.7 us
  transfers between devices with their start and end apart: 5, of which 2 were waited for; matrix products, arithmetic and copies ran while one was open for 24% of the time, Pallas kernels for 0%

commit v1 on v0

--- a/solution.py
+++ b/solution.py
@@ -98,7 +98,12 @@
     ).astype(jnp.bfloat16)
     row_count = normed.shape[0]
     channels = in_weight.shape[2]
-    piece = lax.all_gather(in_weight, "seq", axis=0, tiled=True)
+    ring = [in_weight]
+    for hop_ in range(7):
+        ring.append(lax.ppermute(ring[-1], "seq", [(dev, (dev + 1) % 8) for dev in range(8)]))
+    piece = jnp.roll(
+        jnp.concatenate(ring[::-1], axis=0), (lax.axis_index("seq") + 1) * ring[0].shape[0], axis=0
+    )
     projected = jnp.dot(
         normed, piece.reshape(piece.shape[0], 2 * channels), preferred_element_type=jnp.float32
     )

time: 494 us -> 597 us (1.21)
  waiting for transfers between devices: 151 us -> 197 us
  local copies, waits for them, and re-layouts: 69.2 us -> 106 us
  other arithmetic: 59.8 us -> 88.6 us
  blocking collectives: 174 us -> 163 us
    ppermute x0 -> x7, waiting for transfers between devices: none -> 167 us  [per_device(): lax.ppermute(ring[-1], 'seq', [(dev, (dev + 1) % 8) for dev in range(8)])]
    all_gather x1 -> x0, waiting for transfers between devices: 119 us -> none  [per_device(): piece = lax.all_gather(in_weight, 'seq', axis=0, tiled=True)]
    unnamed x20 -> x55, local copies, waits for them, and re-layouts: 10.5 us -> 38.6 us
    add x16, other arithmetic: 5.87 us -> 16.8 us  [advance(): state = decay * state + key_row[:, None] * (eps_row * drive_row)[None, :]]
    mul x16, other arithmetic: 3.1 us -> 13.8 us  [advance(): product = decay * product]
    all_gather x4, blocking collectives: 139 us -> 131 us  [entering(): everything = jax.tree.map(lambda part: lax.all_gather(part, axis), array)]
    mul x32, other arithmetic: 12.7 us -> 20.4 us  [advance(): decay = 1.0 - eps_row[None, :] * (key_row * key_row)[:, None]]
    dynamic_slice x0 -> x1, local copies, waits for them, and re-layouts: none -> 7.02 us  [per_device(): jnp.roll(jnp.concatenate(ring[::-1], axis=0), (lax.axis_index('seq') + 1)...]
  transfers between devices with their start and end apart: 5 -> 11, of which waited for: 2 -> 9; matrix products, arithmetic and copies ran while one was open for 24% -> 25% of each run, Pallas kernels for 0% -> 0%
where the time goes in v1:
time: 597 us; the launch traced here: 591 us
  waiting for transfers between devices  197 us (33%)
  blocking collectives  163 us (27%)
  local copies, waits for them, and re-layouts  106 us (18%)
  other arithmetic  88.6 us (15%)
  between operations  15.2 us (3%)
  matrix products  10.4 us (2%)
    ppermute x7, waiting for transfers between devices, per_device(): lax.ppermute(ring[-1], 'seq', [(dev, (dev + 1) % 8) for dev in range(8)])  167 us
    all_gather x4, blocking collectives, entering(): everything = jax.tree.map(lambda part: lax.all_gather(part, axis), array)  131 us
    unnamed x55, local copies, waits for them, and re-layouts  38.6 us
    slice x32, local copies, waits for them, and re-layouts, sweep(): lax.scan(advance, (product, initial), (drive_values, key_rows, query_rows...  32.4 us
    psum x1, waiting for transfers between devices, per_device(): features = lax.psum(partial_value, 'chan')  26.4 us
    psum x1, blocking collectives, per_device(): summed = lax.psum(partial_out, 'chan')  25.2 us
    mul x32, other arithmetic, advance(): decay = 1.0 - eps_row[None, :] * (key_row * key_row)[:, None]  20.4 us
    reduce_sum x136, other arithmetic, advance(): output = jnp.sum(query_row[:, None] * state, axis=0)  17.7 us
  transfers between devices with their start and end apart: 11, of which 9 were waited for; matrix products, arithmetic and copies ran while one was open for 25% of the time, Pallas kernels for 0%

profile of v1, /device:TPU:0, one launch (start us, length us, event | category | flops | bytes accessed | tf_op | source)
XLA Modules:
  0.0 591.0 jit_solution(3899246912004150065)
XLA Ops:
  7.4 3.0 collective-permute-start
  10.4 26.4 %collective-permute-done = bf16[256,2,1024]{2,1,0:T(2,128)(2,1)S(1)} collective-permute-done((bf16[256,2,1024]{2,1,0:T(2,128)(2,1)}, bf16[256,2,1024]{2,1,0:T(2,128)(2,1)S(1)}, u32[]{:S(2)}, u32[]{:S(2)}) %collective-permute-start) | collective-permute-done | bytes 1048608 | tf_op jit(solution)/shard_map/ppermute | solution.py:103
  36.8 27.0 %collective-permute-done.1 = bf16[256,2,1024]{2,1,0:T(2,128)(2,1)S(1)} collective-permute-done((bf16[256,2,1024]{2,1,0:T(2,128)(2,1)S(1)}, bf16[256,2,1024]{2,1,0:T(2,128)(2,1)S(1)}, u32[]{:S(2)}, u32[]{:S(2)}) %collective-permute-start.1) | collective-permute-done | bytes 1048608 | tf_op jit(solution)/shard_map/ppermute | solution.py:103
  64.8 26.2 %collective-permute-done.2 = bf16[256,2,1024]{2,1,0:T(2,128)(2,1)S(1)} collective-permute-done((bf16[256,2,1024]{2,1,0:T(2,128)(2,1)S(1)}, bf16[256,2,1024]{2,1,0:T(2,128)(2,1)S(1)}, u32[]{:S(2)}, u32[]{:S(2)}) %collective-permute-start.2) | collective-permute-done | bytes 1048608 | tf_op jit(solution)/shard_map/ppermute | solution.py:103
  92.0 25.3 %collective-permute-done.3 = bf16[256,2,1024]{2,1,0:T(2,128)(2,1)S(1)} collective-permute-done((bf16[256,2,1024]{2,1,0:T(2,128)(2,1)S(1)}, bf16[256,2,1024]{2,1,0:T(2,128)(2,1)S(1)}, u32[]{:S(2)}, u32[]{:S(2)}) %collective-permute-start.3) | collective-permute-done | bytes 1048608 | tf_op jit(solution)/shard_map/ppermute | solution.py:103
  118.3 24.4 %collective-permute-done.4 = bf16[256,2,1024]{2,1,0:T(2,128)(2,1)S(1)} collective-permute-done((bf16[256,2,1024]{2,1,0:T(2,128)(2,1)S(1)}, bf16[256,2,1024]{2,1,0:T(2,128)(2,1)S(1)}, u32[]{:S(2)}, u32[]{:S(2)}) %collective-permute-start.4) | collective-permute-done | bytes 1048608 | tf_op jit(solution)/shard_map/ppermute | solution.py:103
  143.7 23.7 %collective-permute-done.5 = bf16[256,2,1024]{2,1,0:T(2,128)(2,1)} collective-permute-done((bf16[256,2,1024]{2,1,0:T(2,128)(2,1)S(1)}, bf16[256,2,1024]{2,1,0:T(2,128)(2,1)}, u32[]{:S(2)}, u32[]{:S(2)}) %collective-permute-start.5) | collective-permute-done | bytes 1048608 | tf_op jit(solution)/shard_map/ppermute | solution.py:103
  167.5 6.8 %all_gather.30 = bf16[128,2048]{1,0:T(8,128)(2,1)S(1)} all-gather(bf16[128,512]{1,0:T(8,128)(2,1)} %param.22), channel_id=1, replica_groups=mesh['seq'=8,'chan'=4] {'chan'}, dimensions={1}, use_global_device_ids=true | all-gather | bytes 655360 | tf_op jit(solution)/shard_map/all_gather | solution.py:93
  176.3 14.2 %collective-permute-done.6 = bf16[256,2,1024]{2,1,0:T(2,128)(2,1)} collective-permute-done((bf16[256,2,1024]{2,1,0:T(2,128)(2,1)}, bf16[256,2,1024]{2,1,0:T(2,128)(2,1)}, u32[]{:S(2)}, u32[]{:S(2)}) %collective-permute-start.6) | collective-permute-done | bytes 1048608 | tf_op jit(solution)/shard_map/ppermute | solution.py:103
  214.3 7.0 %constant_dynamic-slice_fusion.224 = bf16[2048,2,1024]{2,1,0:T(2,128)(2,1)} fusion(bf16[4096,2,1024]{2,1,0:T(2,128)(2,1)S(1)} %constant_dynamic-update-slice_fusion, s32[]{:T(128)S(6)} %select_n.70), kind=kLoop, calls=%fused_computation.581 | loop fusion | bytes 16777220 | tf_op jit(solution)/shard_map/jit(_roll_dynamic)/dynamic_slice | solution.py:104
  221.3 10.1 %copy.31 = bf16[256,8,2,1024]{3,1,2,0:T(8,128)(2,1)} copy(bf16[256,8,2,1024]{3,2,1,0:T(2,128)(2,1)} %bitcast.855) | data formatting | bytes 16777216
  231.4 4.7 convolution_convert_fusion
  247.5 26.4 %all-reduce.3.cloned.1.call-done = f32[128,2,160]{0,2,1:T(8,128)} async-done(((f32[128,2,160]{0,2,1:T(8,128)}), f32[128,2,160]{0,2,1:T(8,128)}) %all-reduce.3.cloned.1.call-update) | async-done | bytes 163856 | tf_op jit(solution)/shard_map/psum | solution.py:118
  278.8 30.2 %while.90 = (s32[]{:T(128)}, f32[16,1024]{1,0:T(8,128)}, f32[16,1024]{1,0:T(8,128)}, f32[8,16,1024]{2,1,0:T(8,128)S(1)}, f32[8,16,16]{2,1,0:T(8,128)S(1)}, /*ind...) while((s32[]{:T(128)}, f32[16,1024]{1,0:T(8,128)}, ...), condition=%wide.region_4.5_spmd.clone, body=%wide.region_3.4_spmd.clone.sunk | while | flops 2146578 | bytes 924172 | solution.py:67
  309.6 32.3 %all-gather = f32[128,1024]{1,0:T(8,128)S(1)} all-gather(f32[16,1024]{1,0:T(8,128)} %get-tuple-element.565), channel_id=2, replica_groups=mesh['seq'=8,'chan'=4] {'seq'}, dimensions={0}, use_global_device_ids=true | all-gather | bytes 589824 | tf_op jit(solution)/shard_map/all_gather | solution.py:25
  341.9 33.6 %all-gather.1 = f32[128,1024]{1,0:T(8,128)} all-gather(f32[16,1024]{1,0:T(8,128)} %get-tuple-element.566), channel_id=3, replica_groups=mesh['seq'=8,'chan'=4] {'seq'}, dimensions={0}, use_global_device_ids=true | all-gather | bytes 589824 | tf_op jit(solution)/shard_map/all_gather | solution.py:25
  375.6 7.2 %while.91 = (s32[]{:T(128)}, f32[16,1024]{1,0:T(8,128)S(1)}, s32[]{:T(128)}, f32[8,16,1024]{2,1,0:T(8,128)S(1)}, f32[8,16,1024]{2,1,0:T(8,128)}, /*index=5*/s32[]{:T(128)}, s32[]{:T(128)}) while((s32[]{:T(128)}, f32[16,1024]{1,0:T(8,128)S(1)}, s32[]{:T(128)}, f32[8,16,1024]{2,1,0:T(8,128)S(1)}, f32[8,16,1024]{2,1,0:T(8,128)}, ...), condition=%wide.region_6.7_spmd.clone, body=%wide.region_5.6_spmd.clone.sunk | while | flops 65540 | bytes 262245 | solution.py:38
  384.3 22.8 %while.92 = (s32[]{:T(128)}, f32[16,1024]{1,0:T(8,128)S(1)}, f32[16,1024]{1,0:T(8,128)S(1)}, f32[8,16,1024]{2,1,0:T(8,128)}, f32[8,16,16]{2,1,0:T(8,128)S(1)}, /...) while((s32[]{:T(128)}, f32[16,1024]{1,0:T(8,128)S(1)}, ...), condition=%wide.region_26.27_spmd.clone, body=%wide.region_25.26_spmd.clone.sunk | while | flops 2146579 | bytes 924192 | solution.py:67
  407.8 31.5 %all-gather.2 = f32[128,1024]{1,0:T(8,128)S(1)} all-gather(f32[16,1024]{1,0:T(8,128)S(1)} %get-tuple-element.569), channel_id=4, replica_groups=mesh['seq'=8,'chan'=4] {'seq'}, dimensions={0}, use_global_device_ids=true | all-gather | bytes 589824 | tf_op jit(solution)/shard_map/all_gather | solution.py:25
  439.3 33.2 %all-gather.3 = f32[128,1024]{1,0:T(8,128)} all-gather(f32[16,1024]{1,0:T(8,128)S(1)} %get-tuple-element.570), channel_id=5, replica_groups=mesh['seq'=8,'chan'=4] {'seq'}, dimensions={0}, use_global_device_ids=true | all-gather | bytes 589824 | tf_op jit(solution)/shard_map/all_gather | solution.py:25
  472.5 7.3 %while.93 = (s32[]{:T(128)}, f32[16,1024]{1,0:T(8,128)S(1)}, s32[]{:T(128)}, f32[8,16,1024]{2,1,0:T(8,128)S(1)}, f32[8,16,1024]{2,1,0:T(8,128)}, /*index=5*/s32[]{:T(128)}, s32[]{:T(128)}, s32[]{:T(128)}, s32[]{:T(128)}) while((s32[]{:T(128)}, f32[16,1024]{1,0:T(8,128)S(1)}, s32[]{:T(128)}, f32[8,16,1024]{2,1,0:T(8,128)S(1)}, ...), condition=%wide.region_28.29_spmd.clone, body=%wide.region_27.28_spmd.clone.sunk | while | flops 65544 | bytes 262307 | solution.py:38
  480.7 40.1 %while.89 = (s32[]{:T(128)}, f32[16,1024]{1,0:T(8,128)S(1)}, f32[8,16,1024]{2,1,0:T(8,128)}, f32[8,16,1024]{2,1,0:T(8,128)}, f32[8,16,16]{2,1,0:T(8,128)}, /*ind...) while((s32[]{:T(128)}, f32[16,1024]{1,0:T(8,128)S(1)}, ...), condition=%wide.region_46.47_spmd, body=%wide.region_29.46_spmd.sunk | while | flops 2408722 | bytes 2033121 | solution.py:67
  520.8 32.3 %while.88 = (s32[]{:T(128)}, f32[16,1024]{1,0:T(8,128)S(1)}, f32[8,16,1024]{2,1,0:T(8,128)S(1)}, f32[8,16,1024]{2,1,0:T(8,128)S(1)}, f32[8,16,16]{2,1,0:T(8,128)...) while((s32[]{:T(128)}, f32[16,1024]{1,0:T(8,128)S(1)}, ...), condition=%wide.region_24.25_spmd, body=%wide.region_7.24_spmd.sunk | while | flops 2490641 | bytes 2106957 | solution.py:67
  557.6 25.2 %all-reduce.4 = bf16[128,2048]{1,0:T(8,128)(2,1)S(1)} all-reduce(f32[128,2048]{1,0:T(8,128)S(1)} %fusion.342), channel_id=1, replica_groups=mesh['seq'=8,'chan'=4] {'chan'}, use_global_device_ids=true, to_apply=%region_47.48 | all-reduce | flops 262144 | bytes 1572864 | tf_op jit(solution)/shard_map/psum | solution.py:164
  (909 shorter events, 188.6 us)
Async XLA Ops:
  7.4 236.9 %copy-start = (bf16[2,1024,160]{1,2,0:T(8,128)(2,1)S(1)}, bf16[2,1024,160]{1,2,0:T(8,128)(2,1)}, u32[]{:S(2)}) copy-start(bf16[2,1024,160]{1,2,0:T(8,128)(2,1)} %param.27) | copy-start | bytes 1966084
  7.4 206.1 %copy-start.1 = (bf16[256,2,1024]{2,1,0:T(2,128)(2,1)S(1)}, bf16[256,2,1024]{2,1,0:T(2,128)(2,1)}, u32[]{:S(2)}) copy-start(bf16[256,2,1024]{2,1,0:T(2,128)(2,1)} %param.24) | copy-start | bytes 3145732
  7.4 266.6 %all-reduce.3.cloned.1.call-start = ((), (), s32[]{:S(2)}) async-start(), calls=%async_computation | async-start | bytes 327680 | tf_op jit(solution)/shard_map/psum | solution.py:118
  7.4 29.4 %collective-permute-start = (bf16[256,2,1024]{2,1,0:T(2,128)(2,1)}, bf16[256,2,1024]{2,1,0:T(2,128)(2,1)S(1)}, u32[]{:S(2)}, u32[]{:S(2)}) collective-permute-start(bf16[256,2,1024]{2,1,0:T(2,128)(2,1)} %param.24), channel_id=1, source_target_pairs={{0,4},{4,8},{8,12},{12,16},{16,20},{20,24},{24,28},{28,0},{1,5},{5... | collective-permute-start | bytes 3145736 | tf_op jit(solution)/shard_map/ppermute | solution.py:103
  36.8 27.0 %collective-permute-start.1 = (bf16[256,2,1024]{2,1,0:T(2,128)(2,1)S(1)}, bf16[256,2,1024]{2,1,0:T(2,128)(2,1)S(1)}, u32[]{:S(2)}, u32[]{:S(2)}) collective-permute-start(bf16[256,2,1024]{2,1,0:T(2,128)(2,1)S(1)} %collective-permute-done), channel_id=1, source_target_pairs={{0,4},{4,8},{8,12},{12,16},{16,20},{20,24},{24,28},{28,0},{1,5},{5... | collective-permute-start | bytes 3145736 | tf_op jit(solution)/shard_map/ppermute | solution.py:103
  63.8 1.0 copy-start.2
  64.8 26.2 %collective-permute-start.2 = (bf16[256,2,1024]{2,1,0:T(2,128)(2,1)S(1)}, bf16[256,2,1024]{2,1,0:T(2,128)(2,1)S(1)}, u32[]{:S(2)}, u32[]{:S(2)}) collective-permute-start(bf16[256,2,1024]{2,1,0:T(2,128)(2,1)S(1)} %collective-permute-done.1), channel_id=1, source_target_pairs={{0,4},{4,8},{8,12},{12,16},{16,20},{20,24},{24,28},{28,0},{1,5},{5... | collective-permute-start | bytes 3145736 | tf_op jit(solution)/shard_map/ppermute | solution.py:103
  91.0 1.0 copy-start.4
  92.0 25.3 %collective-permute-start.3 = (bf16[256,2,1024]{2,1,0:T(2,128)(2,1)S(1)}, bf16[256,2,1024]{2,1,0:T(2,128)(2,1)S(1)}, u32[]{:S(2)}, u32[]{:S(2)}) collective-permute-start(bf16[256,2,1024]{2,1,0:T(2,128)(2,1)S(1)} %collective-permute-done.2), channel_id=1, source_target_pairs={{0,4},{4,8},{8,12},{12,16},{16,20},{20,24},{24,28},{28,0},{1,5},{5... | collective-permute-start | bytes 3145736 | tf_op jit(solution)/shard_map/ppermute | solution.py:103
  118.3 24.5 %collective-permute-start.4 = (bf16[256,2,1024]{2,1,0:T(2,128)(2,1)S(1)}, bf16[256,2,1024]{2,1,0:T(2,128)(2,1)S(1)}, u32[]{:S(2)}, u32[]{:S(2)}) collective-permute-start(bf16[256,2,1024]{2,1,0:T(2,128)(2,1)S(1)} %collective-permute-done.3), channel_id=1, source_target_pairs={{0,4},{4,8},{8,12},{12,16},{16,20},{20,24},{24,28},{28,0},{1,5},{5... | collective-permute-start | bytes 3145736 | tf_op jit(solution)/shard_map/ppermute | solution.py:103
  143.7 23.7 %collective-permute-start.5 = (bf16[256,2,1024]{2,1,0:T(2,128)(2,1)S(1)}, bf16[256,2,1024]{2,1,0:T(2,128)(2,1)}, u32[]{:S(2)}, u32[]{:S(2)}) collective-permute-start(bf16[256,2,1024]{2,1,0:T(2,128)(2,1)S(1)} %collective-permute-done.4), channel_id=1, source_target_pairs={{0,4},{4,8},{8,12},{12,16},{16,20},{20,24},{24,28},{28,0},{1,5},{5... | collective-permute-start | bytes 3145736 | tf_op jit(solution)/shard_map/ppermute | solution.py:103
  167.4 23.1 %collective-permute-start.6 = (bf16[256,2,1024]{2,1,0:T(2,128)(2,1)}, bf16[256,2,1024]{2,1,0:T(2,128)(2,1)}, u32[]{:S(2)}, u32[]{:S(2)}) collective-permute-start(bf16[256,2,1024]{2,1,0:T(2,128)(2,1)} %collective-permute-done.5), channel_id=1, source_target_pairs={{0,4},{4,8},{8,12},{12,16},{16,20},{20,24},{24,28},{28,0},{1,5},{5... | collective-permute-start | bytes 3145736 | tf_op jit(solution)/shard_map/ppermute | solution.py:103
  167.5 41.8 %copy-start.9 = (bf16[256,2,1024]{2,1,0:T(2,128)(2,1)S(1)}, bf16[256,2,1024]{2,1,0:T(2,128)(2,1)}, u32[]{:S(2)}) copy-start(bf16[256,2,1024]{2,1,0:T(2,128)(2,1)} %copy-done.8) | copy-start | bytes 3145732
  167.5 42.7 %copy-start.7 = (bf16[256,2,1024]{2,1,0:T(2,128)(2,1)S(1)}, bf16[256,2,1024]{2,1,0:T(2,128)(2,1)}, u32[]{:S(2)}) copy-start(bf16[256,2,1024]{2,1,0:T(2,128)(2,1)} %copy-done.6) | copy-start | bytes 3145732
  167.5 43.5 %copy-start.5 = (bf16[256,2,1024]{2,1,0:T(2,128)(2,1)S(1)}, bf16[256,2,1024]{2,1,0:T(2,128)(2,1)}, u32[]{:S(2)}) copy-start(bf16[256,2,1024]{2,1,0:T(2,128)(2,1)} %copy-done.4) | copy-start | bytes 3145732
  167.5 44.3 %copy-start.3 = (bf16[256,2,1024]{2,1,0:T(2,128)(2,1)S(1)}, bf16[256,2,1024]{2,1,0:T(2,128)(2,1)}, u32[]{:S(2)}) copy-start(bf16[256,2,1024]{2,1,0:T(2,128)(2,1)} %copy-done.2) | copy-start | bytes 3145732
  214.3 17.2 %copy-start.12 = (f32[2048]{0:T(1024)S(1)}, f32[2048]{0:T(1024)}, u32[]{:S(2)}) copy-start(f32[2048]{0:T(1024)} %param.23) | copy-start | bytes 24580
  231.4 14.5 %copy-start.15 = (f32[2,1024]{1,0:T(2,128)S(1)}, f32[2,1024]{1,0:T(2,128)}, u32[]{:S(2)}) copy-start(f32[2,1024]{1,0:T(2,128)} %param.29) | copy-start | bytes 24580
  231.4 14.6 %copy-start.16 = (f32[2,1024]{1,0:T(2,128)S(1)}, f32[2,1024]{1,0:T(2,128)}, u32[]{:S(2)}) copy-start(f32[2,1024]{1,0:T(2,128)} %param.30) | copy-start | bytes 24580
  236.6 4.2 collective-permute-start.7
  237.9 5.5 collective-permute-start.8
  245.3 309.4 %all-gather.6.cloned.1.call-start = ((), (), s32[]{:S(2)}) async-start(), calls=%async_computation.1 | async-start | bytes 4718592 | tf_op jit(solution)/shard_map/all_gather | solution.py:161
  384.3 168.8 %copy-start.13 = (f32[1,1024]{1,0:T(1,128)S(1)}, f32[1,1024]{1,0:T(1,128)}, u32[]{:S(2)}) copy-start(f32[1,1024]{1,0:T(1,128)} %get-tuple-element.1292) | copy-start | bytes 12292
  384.3 168.8 %copy-start.14 = (f32[1,1024]{1,0:T(1,128)S(1)}, f32[1,1024]{1,0:T(1,128)}, u32[]{:S(2)}) copy-start(f32[1,1024]{1,0:T(1,128)} %get-tuple-element.1293) | copy-start | bytes 12292
  (4 other events, 3.2 us)
Sparse Core Ops, SparseCore 0:
  245.5 28.4 all-reduce.2
Sparse Core Ops, SparseCore 1:
  247.9 72.5 all-gather.5
